TPU v7x, 256 devices: a whole 4x4x8 slice. The times are simulated.
256 devices in a mesh: section: 2 (over x_hi), feat: 16 (over y, x_lo, core), width: 8 (over z).
Axes of the slice: x: 4 (x_hi: 2, x_lo: 2; x = x_hi * 2 + x_lo), y: 4, z: 8, core: 2. Of those that a mesh axis runs over, the one named last changes fastest.
Arguments:
- mlp_inputs: bfloat16 [4, 1024, 2304], P('section', 'width'), may hold values from -6 to 6
- encoder: bfloat16 [4, 2304, 16384], P('section', 'width', 'feat'), may hold values from -0.125 to 0.125
- enc_bias: float32 [4, 16384], P('section', 'feat'), may hold values from -3 to 3
- decoder: bfloat16 [10, 16384, 2304], P('section', 'feat', 'width'), may hold values from -0.046875 to 0.046875
- dec_bias: float32 [4, 2304], P(None, 'width'), may hold values from -3 to 3
- targets: bfloat16 [4, 1024, 2304], P(None, None, 'width'), may hold values from -6 to 6
- live_rows: int32 [1024], replicated, may hold values 0 or 1
Outputs:
- errors: bfloat16 [4, 1024, 2304], P(None, None, 'width')
- gradients: bfloat16 [10, 16384, 2304], P('section', 'feat', 'width')
All inputs are finite; a program needn't handle non-finite values.
Results may differ from a plain program's by a relative error of at most 0.0042.
Values may be sent and summed in bfloat16 or wider, within the bound.
No kernel may reach another device: no remote copies, remote signals or barrier semaphores. Data moves between devices by JAX's collectives and lax.ppermute only.
A program may use at most 128 MiB of HBM per device.

v0:
```python
import jax
import jax.numpy as jnp
from jax import lax
from jax.sharding import PartitionSpec as P


def from_behind(value, axis, steps):
    count = lax.axis_size(axis)
    initial, last = (max(0, -steps), min(count, count - steps))
    return lax.ppermute(value, axis, [(source, source + steps) for source in range(initial, last)])


def pair_tables(layer_count):
    source_ids = []
    target_ids = []
    for source in range(layer_count):
        for target in range(source, layer_count):
            source_ids.append(source)
            target_ids.append(target)
    return (jnp.array(source_ids, jnp.int32), jnp.array(target_ids, jnp.int32))


def local(mlp_inputs, encoder, enc_bias, decoder, dec_bias, targets, live_rows):
    layers_here, tok_local, model_width = mlp_inputs.shape
    pre_act = jnp.einsum(
        "ltd,ldf->tlf",
        mlp_inputs,
        lax.all_gather(encoder, "width", axis=1, tiled=True),
        preferred_element_type=jnp.float32,
    )
    local_feats = jnp.maximum(pre_act + enc_bias[None, :, :], 0.0).astype(jnp.bfloat16)
    token_feats = lax.all_gather(local_feats, "width", axis=0, tiled=True)
    layers_all = dec_bias.shape[0]
    tokens_all = live_rows.shape[0]
    per_section = decoder.shape[0]
    source_ids, target_ids = pair_tables(layers_all)
    section_id = lax.axis_index("section")
    earlier = from_behind(token_feats[:, layers_here - 1], "section", 1)
    features = jnp.concatenate([earlier[:, None, :], token_feats], axis=1)
    first_layer = section_id * layers_here - 1
    rebuilt = jnp.zeros((layers_all, tokens_all, decoder.shape[2]), jnp.float32)
    chosen = []
    for pair_slot in range(per_section):
        pair_id = section_id * per_section + pair_slot
        source = source_ids[pair_id]
        target = target_ids[pair_id]
        picked = lax.dynamic_index_in_dim(features, source - first_layer, 1, keepdims=False)
        chosen.append((picked, target))
        partial_value = jnp.dot(picked, decoder[pair_slot], preferred_element_type=jnp.float32)
        current = lax.dynamic_index_in_dim(rebuilt, target, 0, keepdims=False)
        rebuilt = lax.dynamic_update_index_in_dim(rebuilt, current + partial_value, target, 0)
    summed = lax.psum(rebuilt, ("section", "feat"))
    keep_rows = live_rows.astype(jnp.float32)[None, :, None]
    errors = ((summed + dec_bias[:, None, :] - targets.astype(jnp.float32)) * keep_rows).astype(
        jnp.bfloat16
    )
    gradients = []
    for picked, target in chosen:
        residual = lax.dynamic_index_in_dim(errors, target, 0, keepdims=False)
        product = lax.dot_general(
            picked, residual, (((0,), (0,)), ((), ())), preferred_element_type=jnp.float32
        )
        gradients.append((product / tokens_all).astype(jnp.bfloat16))
    return (errors, jnp.stack(gradients))


def solution(mesh):
    placed = (
        P("section", "width", None),
        P("section", "width", "feat"),
        P("section", "feat"),
        P("section", "feat", "width"),
        P(None, "width"),
        P(None, None, "width"),
        P(),
    )
    return jax.shard_map(
        local,
        mesh=mesh,
        in_specs=placed,
        out_specs=(P(None, None, "width"), P("section", "feat", "width")),
        check_vma=False,
    )
```

profile of v0, /device:TPU:1, one launch (start us, length us, event | category | flops | bytes accessed | tf_op | source)
XLA Modules:
  0.0 397.8 jit_solution(8431505922366384273)
XLA Ops:
  8.0 109.4 %all-gather.3.cloned.1.call-done = bf16[2,2304,1024]{2,1,0:T(8,128)(2,1)} async-done(((bf16[2,288,1024]{2,1,0:T(8,128)(2,1)}), bf16[2,2304,1024]{2,1,0:T(8,128)(2,1)}) %all-gather.3.cloned.1.call-update) | async-done | bytes 9437200 | tf_op jit(solution)/shard_map/all_gather | solution.py:28
  117.3 7.3 %fusion.36 = bf16[128,2,1024]{0,2,1:T(8,128)(2,1)} fusion(bf16[2,2304,1024]{2,1,0:T(8,128)(2,1)} %all-gather.3.cloned.1.call-done, bf16[2,128,2304]{2,1,0:T(8,128)(2,1)S(1)} %copy-done, f32[2,1024]{1,0:T(2,128)} %param.11), kind=kOutput, calls=%fused_computation.59 | convolution fusion | flops 1208745984 | bytes 11149312 | tf_op jit(solution)/shard_map/ltd,ldf->tlf/dot_general | solution.py:25
  124.7 57.6 %all-gather.5.cloned.1.call-done = bf16[1024,2,1024]{0,2,1:T(8,128)(2,1)} async-done(((bf16[128,2,1024]{0,2,1:T(8,128)(2,1)}), bf16[1024,2,1024]{0,2,1:T(8,128)(2,1)}) %all-gather.5.cloned.1.call-update) | async-done | bytes 4194320 | tf_op jit(solution)/shard_map/all_gather | solution.py:32
  182.4 3.1 slice_bitcast_fusion
  185.4 4.4 %collective-permute-start = (bf16[1024,1024]{0,1:T(8,128)(2,1)}, bf16[1024,1024]{0,1:T(8,128)(2,1)S(1)}, u32[]{:S(2)}, u32[]{:S(2)}) collective-permute-start(bf16[1024,1024]{0,1:T(8,128)(2,1)} %slice_bitcast_fusion), channel_id=1, source_target_pairs={{0,128},{1,129},{2,130},{3,131},{4,132},{5,133},{6,134},{7,135},{8... | collective-permute-start | bytes 6291464 | tf_op jit(solution)/shard_map/ppermute | solution.py:10
  203.2 26.7 %collective-permute-done = bf16[1024,1024]{0,1:T(8,128)(2,1)S(1)} collective-permute-done((bf16[1024,1024]{0,1:T(8,128)(2,1)}, bf16[1024,1024]{0,1:T(8,128)(2,1)S(1)}, u32[]{:S(2)}, u32[]{:S(2)}) %collective-permute-start) | collective-permute-done | bytes 2097184 | tf_op jit(solution)/shard_map/ppermute | solution.py:10
  229.9 3.0 broadcast_in_dim.25
  233.7 3.4 fusion.18
  237.1 1.3 constant_dynamic-slice_fusion.3
  238.5 2.2 fusion.17
  240.7 1.3 constant_dynamic-slice_fusion.2
  242.1 2.2 fusion.15
  244.3 1.3 constant_dynamic-slice_fusion.1
  245.6 2.3 fusion.13
  247.9 1.3 constant_dynamic-slice_fusion
  249.3 2.2 fusion.11
  252.2 126.4 %all-reduce.2.cloned.1.call-done = f32[4,1024,288]{1,2,0:T(8,128)} async-done(((f32[4,1024,288]{1,2,0:T(8,128)}), f32[4,1024,288]{1,2,0:T(8,128)}) %all-reduce.2.cloned.1.call-update) | async-done | bytes 4718608 | tf_op jit(solution)/shard_map/psum | solution.py:52
  378.6 3.9 multiply_convert_fusion
  382.8 1.4 fusion.35
  384.2 1.4 fusion.33
  385.6 1.4 fusion.31
  386.9 1.4 fusion.29
  388.3 1.4 fusion.27
  389.7 1.6 copy-done.9
  (27 shorter events, 3.4 us)
Async XLA Ops:
  7.2 110.2 %copy-start = (bf16[2,128,2304]{2,1,0:T(8,128)(2,1)S(1)}, bf16[2,128,2304]{2,1,0:T(8,128)(2,1)}, u32[]{:S(2)}) copy-start(bf16[2,128,2304]{2,1,0:T(8,128)(2,1)} %param.9) | copy-start | bytes 3538948
  7.2 110.2 %all-gather.3.cloned.1.call-start = ((), (), s32[]{:S(2)}) async-start(), calls=%async_computation | async-start | bytes 10616832 | tf_op jit(solution)/shard_map/all_gather | solution.py:28
  7.9 174.4 %all-gather.5.cloned.1.call-start = ((), (), s32[]{:S(2)}) async-start(), calls=%async_computation.1 | async-start | bytes 4718592 | tf_op jit(solution)/shard_map/all_gather | solution.py:32
  124.7 65.2 %copy-start.5 = (s32[10]{0:T(128)S(1)}, s32[10]{0:T(128)}, u32[]{:S(2)}) copy-start(s32[10]{0:T(128)} %constant.92.clone) | copy-start | bytes 124
  124.7 65.2 %copy-start.6 = (s32[10]{0:T(128)S(1)}, s32[10]{0:T(128)}, u32[]{:S(2)}) copy-start(s32[10]{0:T(128)} %constant.93.clone) | copy-start | bytes 124
  124.7 253.9 %all-reduce.2.cloned.1.call-start = ((), (), s32[]{:S(2)}) async-start(), calls=%async_computation.2 | async-start | bytes 9437184 | tf_op jit(solution)/shard_map/psum | solution.py:52
  185.4 44.5 %collective-permute-start = (bf16[1024,1024]{0,1:T(8,128)(2,1)}, bf16[1024,1024]{0,1:T(8,128)(2,1)S(1)}, u32[]{:S(2)}, u32[]{:S(2)}) collective-permute-start(bf16[1024,1024]{0,1:T(8,128)(2,1)} %slice_bitcast_fusion), channel_id=1, source_target_pairs={{0,128},{1,129},{2,130},{3,131},{4,132},{5,133},{6,134},{7,135},{8... | collective-permute-start | bytes 6291464 | tf_op jit(solution)/shard_map/ppermute | solution.py:10
  229.9 3.8 copy-start.1
  233.7 4.7 %copy-start.3 = (bf16[5,1024,288]{1,2,0:T(8,128)(2,1)S(1)}, bf16[5,1024,288]{1,2,0:T(8,128)(2,1)}, u32[]{:S(2)}) copy-start(bf16[5,1024,288]{1,2,0:T(8,128)(2,1)} %param.12) | copy-start | bytes 8847364
  251.5 0.7 copy-start.8
  251.5 127.1 %copy-start.7 = (f32[4,288]{1,0:T(4,128)S(1)}, f32[4,288]{1,0:T(4,128)}, u32[]{:S(2)}) copy-start(f32[4,288]{1,0:T(4,128)} %param.13) | copy-start | bytes 13828
  378.6 4.2 %copy-start.2 = (bf16[1024,2,1024]{0,2,1:T(8,128)(2,1)S(1)}, bf16[1024,2,1024]{0,2,1:T(8,128)(2,1)}, u32[]{:S(2)}) copy-start(bf16[1024,2,1024]{0,2,1:T(8,128)(2,1)} %all-gather.5.cloned.1.call-done) | copy-start | bytes 12582916
  382.8 5.5 %copy-start.4 = (bf16[4,1024,288]{1,2,0:T(8,128)(2,1)}, bf16[4,1024,288]{1,2,0:T(8,128)(2,1)S(1)}, u32[]{:S(2)}) copy-start(bf16[4,1024,288]{1,2,0:T(8,128)(2,1)S(1)} %multiply_convert_fusion) | copy-start | bytes 7077892
  389.7 1.6 copy-start.9
Sparse Core Ops, SparseCore 0:
  9.8 107.5 all-gather.2
  124.8 57.5 all-gather.4
  251.6 126.9 all-reduce.1
where the time goes:
time: 398 us
  waiting for transfers between devices  321 us (81%)
  matrix products  26.5 us (7%)
  between operations  26.5 us (7%)
  local copies, waits for them, and re-layouts  15.5 us (4%)
  starting transfers between devices  4.52 us (1%)
    psum x1, waiting for transfers between devices, local(): summed = lax.psum(rebuilt, ('section', 'feat'))  126 us
    all_gather x1, waiting for transfers between devices, local(): lax.all_gather(encoder, 'width', axis=1, tiled=True)  109 us
    all_gather x1, waiting for transfers between devices, local(): token_feats = lax.all_gather(local_feats, 'width', axis=0, tiled=True)  57.6 us
    ppermute x1, waiting for transfers between devices, from_behind(): lax.ppermute(value, axis, [(source, source + steps) for source in range(i...  26.7 us
    dot_general x5, matrix products, local(): jnp.dot(picked, decoder[pair_slot], preferred_element_type=jnp.float32)  12.3 us
  transfers between devices with their start and end apart: 4, of which 4 were waited for; matrix products, arithmetic and copies ran while one was open for 0% of the time, Pallas kernels for 0%

commit v1 on v0

--- a/solution.py
+++ b/solution.py
@@ -22,12 +22,38 @@
 
 def local(mlp_inputs, encoder, enc_bias, decoder, dec_bias, targets, live_rows):
     layers_here, tok_local, model_width = mlp_inputs.shape
-    pre_act = jnp.einsum(
+    count_2, here, rows = (lax.axis_size("width"), lax.axis_index("width"), encoder.shape[1])
+    right = [(i, (i + 1) % count_2) for i in range(count_2)]
+    left = [(i, (i - 1) % count_2) for i in range(count_2)]
+    half = count_2 // 2
+    from_left = from_right = encoder
+    total = jnp.einsum(
         "ltd,ldf->tlf",
-        mlp_inputs,
-        lax.all_gather(encoder, "width", axis=1, tiled=True),
+        lax.dynamic_slice_in_dim(mlp_inputs, here * rows, encoder.shape[1], axis=2),
+        encoder,
         preferred_element_type=jnp.float32,
     )
+    for step in range(1, half + 1):
+        from_left = lax.ppermute(from_left, "width", right)
+        if step < count_2 - half:
+            from_right = lax.ppermute(from_right, "width", left)
+            total = total + jnp.einsum(
+                "ltd,ldf->tlf",
+                lax.dynamic_slice_in_dim(
+                    mlp_inputs, (here + step) % count_2 * rows, from_right.shape[1], axis=2
+                ),
+                from_right,
+                preferred_element_type=jnp.float32,
+            )
+        total = total + jnp.einsum(
+            "ltd,ldf->tlf",
+            lax.dynamic_slice_in_dim(
+                mlp_inputs, (here - step) % count_2 * rows, from_left.shape[1], axis=2
+            ),
+            from_left,
+            preferred_element_type=jnp.float32,
+        )
+    pre_act = total
     local_feats = jnp.maximum(pre_act + enc_bias[None, :, :], 0.0).astype(jnp.bfloat16)
     token_feats = lax.all_gather(local_feats, "width", axis=0, tiled=True)
     layers_all = dec_bias.shape[0]

time: 398 us -> 396 us (level)
  waiting for transfers between devices: 321 us -> 303 us
  starting transfers between devices: 4.52 us -> 17 us
    all_gather x1 -> x0, waiting for transfers between devices: 109 us -> none  [local(): lax.all_gather(encoder, 'width', axis=1, tiled=True)]
    ppermute x0 -> x7, waiting for transfers between devices: none -> 92.3 us  [the longest x4 92.3 us: local(): from_left = lax.ppermute(from_left, 'width', right)]
    ppermute x0 -> x7, starting transfers between devices: none -> 12 us  [the longest x3 9.45 us: local(): from_right = lax.ppermute(from_right, 'width', left)]
    dot_general x1 -> x8, matrix products: 7.31 us -> 9.79 us  [the longest x4 5.28 us: local(): jnp.einsum('ltd,ldf->tlf', lax.dynamic_slice_in_dim(mlp_inputs, (here - s...]
  transfers between devices with their start and end apart: 4 -> 10, of which waited for: 4 -> 7; matrix products, arithmetic and copies ran while one was open for 0% -> 2% of each run, Pallas kernels for 0% -> 0%
where the time goes in v1:
time: 396 us; the launch traced here: 395 us
  waiting for transfers between devices  303 us (77%)
  matrix products  29.2 us (7%)
  between operations  27.3 us (7%)
  starting transfers between devices  17 us (4%)
  local copies, waits for them, and re-layouts  15.6 us (4%)
    psum x1, waiting for transfers between devices, local(): summed = lax.psum(rebuilt, ('section', 'feat'))  123 us
    ppermute x4, waiting for transfers between devices, local(): from_left = lax.ppermute(from_left, 'width', right)  92.3 us
    all_gather x1, waiting for transfers between devices, local(): token_feats = lax.all_gather(local_feats, 'width', axis=0, tiled=True)  57 us
    ppermute x1, waiting for transfers between devices, from_behind(): lax.ppermute(value, axis, [(source, source + steps) for source in range(i...  30.3 us
    dot_general x5, matrix products, local(): jnp.dot(picked, decoder[pair_slot], preferred_element_type=jnp.float32)  13.5 us
    ppermute x3, starting transfers between devices, local(): from_right = lax.ppermute(from_right, 'width', left)  9.45 us
  transfers between devices with their start and end apart: 10, of which 7 were waited for; matrix products, arithmetic and copies ran while one was open for 2% of the time, Pallas kernels for 0%

profile of v1, /device:TPU:1, one launch (start us, length us, event | category | flops | bytes accessed | tf_op | source)
XLA Modules:
  0.0 395.5 jit_solution(12592207837010925702)
XLA Ops:
  7.2 2.5 collective-permute-start.1
  9.8 4.0 %collective-permute-start = (bf16[2,288,1024]{2,1,0:T(8,128)(2,1)}, bf16[2,288,1024]{2,1,0:T(8,128)(2,1)}, u32[]{:S(2)}, u32[]{:S(2)}) collective-permute-start(bf16[2,288,1024]{2,1,0:T(8,128)(2,1)} %param.10), channel_id=1, source_target_pairs={{0,7},{1,0},{2,1},{3,2},{4,3},{5,4},{6,5},{7,6},{8,15},{9,8},{10,9... | collective-permute-start | bytes 3538952 | tf_op jit(solution)/shard_map/ppermute | solution.py:39
  13.8 25.8 %collective-permute-done.1 = bf16[2,288,1024]{2,1,0:T(8,128)(2,1)S(1)} collective-permute-done((bf16[2,288,1024]{2,1,0:T(8,128)(2,1)}, bf16[2,288,1024]{2,1,0:T(8,128)(2,1)S(1)}, u32[]{:S(2)}, u32[]{:S(2)}) %collective-permute-start.1) | collective-permute-done | bytes 1179680 | tf_op jit(solution)/shard_map/ppermute | solution.py:37
  39.6 2.7 collective-permute-start.2
  42.3 24.9 %collective-permute-done.3 = bf16[2,288,1024]{2,1,0:T(8,128)(2,1)} collective-permute-done((bf16[2,288,1024]{2,1,0:T(8,128)(2,1)S(1)}, bf16[2,288,1024]{2,1,0:T(8,128)(2,1)}, u32[]{:S(2)}, u32[]{:S(2)}) %collective-permute-start.3) | collective-permute-done | bytes 1179680 | tf_op jit(solution)/shard_map/ppermute | solution.py:37
  67.2 1.7 fusion.69
  68.9 1.8 convolution_add_fusion.8
  70.7 2.8 collective-permute-start.4
  74.0 20.2 %collective-permute-done.5 = bf16[2,288,1024]{2,1,0:T(8,128)(2,1)} collective-permute-done((bf16[2,288,1024]{2,1,0:T(8,128)(2,1)}, bf16[2,288,1024]{2,1,0:T(8,128)(2,1)}, u32[]{:S(2)}, u32[]{:S(2)}) %collective-permute-start.5) | collective-permute-done | bytes 1179680 | tf_op jit(solution)/shard_map/ppermute | solution.py:37
  94.1 1.8 fusion.64
  96.4 1.8 fusion.61
  98.7 21.4 %collective-permute-done.6 = bf16[2,288,1024]{2,1,0:T(8,128)(2,1)S(1)} collective-permute-done((bf16[2,288,1024]{2,1,0:T(8,128)(2,1)}, bf16[2,288,1024]{2,1,0:T(8,128)(2,1)S(1)}, u32[]{:S(2)}, u32[]{:S(2)}) %collective-permute-start.6) | collective-permute-done | bytes 1179680 | tf_op jit(solution)/shard_map/ppermute | solution.py:37
  121.5 57.0 %all-gather.2.cloned.1.call-done = bf16[1024,2,1024]{2,0,1:T(8,128)(2,1)} async-done(((bf16[128,2,1024]{2,0,1:T(8,128)(2,1)}), bf16[1024,2,1024]{2,0,1:T(8,128)(2,1)}) %all-gather.2.cloned.1.call-update) | async-done | bytes 4194320 | tf_op jit(solution)/shard_map/all_gather | solution.py:58
  178.5 3.1 slice_bitcast_fusion
  181.6 4.9 %collective-permute-start.7 = (bf16[1024,1024]{1,0:T(8,128)(2,1)}, bf16[1024,1024]{1,0:T(8,128)(2,1)S(1)}, u32[]{:S(2)}, u32[]{:S(2)}) collective-permute-start(bf16[1024,1024]{1,0:T(8,128)(2,1)} %slice_bitcast_fusion), channel_id=1, source_target_pairs={{0,128},{1,129},{2,130},{3,131},{4,132},{5,133},{6,134},{7,135},{8... | collective-permute-start | bytes 6291464 | tf_op jit(solution)/shard_map/ppermute | solution.py:10
  200.3 30.3 %collective-permute-done.7 = bf16[1024,1024]{1,0:T(8,128)(2,1)S(1)} collective-permute-done((bf16[1024,1024]{1,0:T(8,128)(2,1)}, bf16[1024,1024]{1,0:T(8,128)(2,1)S(1)}, u32[]{:S(2)}, u32[]{:S(2)}) %collective-permute-start.7) | collective-permute-done | bytes 2097184 | tf_op jit(solution)/shard_map/ppermute | solution.py:10
  230.7 3.0 broadcast_in_dim.25
  234.5 3.6 fusion.18
  239.4 2.4 fusion.17
  243.2 2.5 fusion.15
  247.0 2.5 fusion.13
  250.9 2.5 fusion.11
  254.0 122.8 %all-reduce.2.cloned.1.call-done = f32[4,1024,288]{1,2,0:T(8,128)} async-done(((f32[4,1024,288]{1,2,0:T(8,128)}), f32[4,1024,288]{1,2,0:T(8,128)}) %all-reduce.2.cloned.1.call-update) | async-done | bytes 4718608 | tf_op jit(solution)/shard_map/psum | solution.py:78
  376.8 3.9 multiply_convert_fusion
  (47 shorter events, 18.3 us)
Async XLA Ops:
  7.2 60.0 %copy-start = (bf16[2,128,2304]{2,1,0:T(8,128)(2,1)S(1)}, bf16[2,128,2304]{2,1,0:T(8,128)(2,1)}, u32[]{:S(2)}) copy-start(bf16[2,128,2304]{2,1,0:T(8,128)(2,1)} %param.9) | copy-start | bytes 3538948
  7.2 171.4 %all-gather.2.cloned.1.call-start = ((), (), s32[]{:S(2)}) async-start(), calls=%async_computation | async-start | bytes 4718592 | tf_op jit(solution)/shard_map/all_gather | solution.py:58
  7.2 32.4 %collective-permute-start.1 = (bf16[2,288,1024]{2,1,0:T(8,128)(2,1)}, bf16[2,288,1024]{2,1,0:T(8,128)(2,1)S(1)}, u32[]{:S(2)}, u32[]{:S(2)}) collective-permute-start(bf16[2,288,1024]{2,1,0:T(8,128)(2,1)} %param.10), channel_id=1, source_target_pairs={{0,1},{1,2},{2,3},{3,4},{4,5},{5,6},{6,7},{7,0},{8,9},{9,10},{10,1... | collective-permute-start | bytes 3538952 | tf_op jit(solution)/shard_map/ppermute | solution.py:37
  9.8 29.8 %collective-permute-start = (bf16[2,288,1024]{2,1,0:T(8,128)(2,1)}, bf16[2,288,1024]{2,1,0:T(8,128)(2,1)}, u32[]{:S(2)}, u32[]{:S(2)}) collective-permute-start(bf16[2,288,1024]{2,1,0:T(8,128)(2,1)} %param.10), channel_id=1, source_target_pairs={{0,7},{1,0},{2,1},{3,2},{4,3},{5,4},{6,5},{7,6},{8,15},{9,8},{10,9... | collective-permute-start | bytes 3538952 | tf_op jit(solution)/shard_map/ppermute | solution.py:39
  39.6 27.6 %collective-permute-start.3 = (bf16[2,288,1024]{2,1,0:T(8,128)(2,1)S(1)}, bf16[2,288,1024]{2,1,0:T(8,128)(2,1)}, u32[]{:S(2)}, u32[]{:S(2)}) collective-permute-start(bf16[2,288,1024]{2,1,0:T(8,128)(2,1)S(1)} %collective-permute-done.1), channel_id=1, source_target_pairs={{0,1},{1,2},{2,3},{3,4},{4,5},{5,6},{6,7},{7,0},{8,9},{9,10},{10,1... | collective-permute-start | bytes 3538952 | tf_op jit(solution)/shard_map/ppermute | solution.py:37
  39.6 31.1 %collective-permute-start.2 = (bf16[2,288,1024]{2,1,0:T(8,128)(2,1)}, bf16[2,288,1024]{2,1,0:T(8,128)(2,1)S(1)}, u32[]{:S(2)}, u32[]{:S(2)}) collective-permute-start(bf16[2,288,1024]{2,1,0:T(8,128)(2,1)} %collective-permute-done), channel_id=1, source_target_pairs={{0,7},{1,0},{2,1},{3,2},{4,3},{5,4},{6,5},{7,6},{8,15},{9,8},{10,9... | collective-permute-start | bytes 3538952 | tf_op jit(solution)/shard_map/ppermute | solution.py:39
  67.2 26.9 %collective-permute-start.5 = (bf16[2,288,1024]{2,1,0:T(8,128)(2,1)}, bf16[2,288,1024]{2,1,0:T(8,128)(2,1)}, u32[]{:S(2)}, u32[]{:S(2)}) collective-permute-start(bf16[2,288,1024]{2,1,0:T(8,128)(2,1)} %collective-permute-done.3), channel_id=1, source_target_pairs={{0,1},{1,2},{2,3},{3,4},{4,5},{5,6},{6,7},{7,0},{8,9},{9,10},{10,1... | collective-permute-start | bytes 3538952 | tf_op jit(solution)/shard_map/ppermute | solution.py:37
  70.7 27.5 %collective-permute-start.4 = (bf16[2,288,1024]{2,1,0:T(8,128)(2,1)S(1)}, bf16[2,288,1024]{2,1,0:T(8,128)(2,1)S(1)}, u32[]{:S(2)}, u32[]{:S(2)}) collective-permute-start(bf16[2,288,1024]{2,1,0:T(8,128)(2,1)S(1)} %collective-permute-done.2), channel_id=1, source_target_pairs={{0,7},{1,0},{2,1},{3,2},{4,3},{5,4},{6,5},{7,6},{8,15},{9,8},{10,9... | collective-permute-start | bytes 3538952 | tf_op jit(solution)/shard_map/ppermute | solution.py:39
  94.1 26.0 %collective-permute-start.6 = (bf16[2,288,1024]{2,1,0:T(8,128)(2,1)}, bf16[2,288,1024]{2,1,0:T(8,128)(2,1)S(1)}, u32[]{:S(2)}, u32[]{:S(2)}) collective-permute-start(bf16[2,288,1024]{2,1,0:T(8,128)(2,1)} %collective-permute-done.5), channel_id=1, source_target_pairs={{0,1},{1,2},{2,3},{3,4},{4,5},{5,6},{6,7},{7,0},{8,9},{9,10},{10,1... | collective-permute-start | bytes 3538952 | tf_op jit(solution)/shard_map/ppermute | solution.py:37
  98.2 21.9 %copy-start.7 = (f32[2,1024]{1,0:T(2,128)S(1)}, f32[2,1024]{1,0:T(2,128)}, u32[]{:S(2)}) copy-start(f32[2,1024]{1,0:T(2,128)} %param.11) | copy-start | bytes 24580
  121.4 65.1 %copy-start.5 = (s32[10]{0:T(128)S(1)}, s32[10]{0:T(128)}, u32[]{:S(2)}) copy-start(s32[10]{0:T(128)} %constant.142.clone) | copy-start | bytes 124
  121.4 65.1 %copy-start.6 = (s32[10]{0:T(128)S(1)}, s32[10]{0:T(128)}, u32[]{:S(2)}) copy-start(s32[10]{0:T(128)} %constant.143.clone) | copy-start | bytes 124
  121.4 255.4 %all-reduce.2.cloned.1.call-start = ((), (), s32[]{:S(2)}) async-start(), calls=%async_computation.1 | async-start | bytes 9437184 | tf_op jit(solution)/shard_map/psum | solution.py:78
  181.6 49.0 %collective-permute-start.7 = (bf16[1024,1024]{1,0:T(8,128)(2,1)}, bf16[1024,1024]{1,0:T(8,128)(2,1)S(1)}, u32[]{:S(2)}, u32[]{:S(2)}) collective-permute-start(bf16[1024,1024]{1,0:T(8,128)(2,1)} %slice_bitcast_fusion), channel_id=1, source_target_pairs={{0,128},{1,129},{2,130},{3,131},{4,132},{5,133},{6,134},{7,135},{8... | collective-permute-start | bytes 6291464 | tf_op jit(solution)/shard_map/ppermute | solution.py:10
  230.7 3.8 copy-start.1
  234.5 5.0 %copy-start.4 = (bf16[5,1024,288]{1,2,0:T(8,128)(2,1)S(1)}, bf16[5,1024,288]{1,2,0:T(8,128)(2,1)}, u32[]{:S(2)}) copy-start(bf16[5,1024,288]{1,2,0:T(8,128)(2,1)} %param.12) | copy-start | bytes 8847364
  253.4 0.7 copy-start.9
  253.4 123.5 %copy-start.8 = (f32[4,288]{1,0:T(4,128)S(1)}, f32[4,288]{1,0:T(4,128)}, u32[]{:S(2)}) copy-start(f32[4,288]{1,0:T(4,128)} %param.13) | copy-start | bytes 13828
  376.8 4.2 %copy-start.2 = (bf16[1024,2,1024]{2,0,1:T(8,128)(2,1)S(1)}, bf16[1024,2,1024]{2,0,1:T(8,128)(2,1)}, u32[]{:S(2)}) copy-start(bf16[1024,2,1024]{2,0,1:T(8,128)(2,1)} %all-gather.2.cloned.1.call-done) | copy-start | bytes 12582916
  381.1 4.7 %copy-start.3 = (bf16[4,1024,288]{1,2,0:T(8,128)(2,1)}, bf16[4,1024,288]{1,2,0:T(8,128)(2,1)S(1)}, u32[]{:S(2)}) copy-start(bf16[4,1024,288]{1,2,0:T(8,128)(2,1)S(1)} %multiply_convert_fusion) | copy-start | bytes 7077892
  387.0 1.6 copy-start.10
Sparse Core Ops, SparseCore 0:
  121.5 56.9 all-gather.1
  253.5 123.2 all-reduce.1
